TPU v7x, 32 devices: a whole 2x2x4 slice. The times are simulated.
32 devices in a mesh: gx: 2 (over x), gy: 4 (over z), gz: 4 (over y, core).
Axes of the slice: x: 2, y: 2, z: 4, core: 2. Of those that a mesh axis runs over, the one named last changes fastest.
Arguments:
- particle_mass: float32 [1048576], P(('gx', 'gy', 'gz')), may hold values from 0.5 to 2
- particle_velocity: float32 [3, 1048576], P(None, ('gx', 'gy', 'gz')), may hold values from -6 to 6
- particle_affine: float32 [9, 1048576], P(None, ('gx', 'gy', 'gz')), may hold values from -6 to 6
- particle_cell: int32 [3, 1048576], P(None, ('gx', 'gy', 'gz')), may hold values from 0 to 13
- particle_fraction: int32 [3, 1048576], P(None, ('gx', 'gy', 'gz')), may hold values from 0 to 1023
- block_owner: int32 [2048, 1], P(('gx', 'gy', 'gz')), may hold values from 0 to 15; in each aligned block of 64 rows (0 to 63, 64 to 127, ...) at most 8 rows name the same one
- block_slot: int32 [2048], P(('gx', 'gy', 'gz')), may hold values from 0 to 31
- block_count: int32 [2048], P(('gx', 'gy', 'gz')), may hold values from 128 to 512
- cell_drag: float32 [1024, 4096], P(('gx', 'gy', 'gz')), may hold values from 0.5 to 2
Outputs:
- grid_velocity: float32 [1024, 3, 4096], P(('gx', 'gy', 'gz'))
- new_velocity: float32 [3, 1048576], P(None, ('gx', 'gy', 'gz'))
- new_affine: float32 [9, 1048576], P(None, ('gx', 'gy', 'gz'))
Inputs may be any that keep to these rules, and one draw needn't show every extreme that they name: `block_owner`: owner index counted over the devices with the particle device's own gx index, in gy+gz order; among the rows of one device, no owner is named more than 8 times. `block_count`: slots at or beyond the count are absent. `particle_cell`: A particle's three stencil nodes lie inside its grid block.
All inputs are finite; a program needn't handle non-finite values.
Results may differ from a plain program's by a relative error of at most 0.0085.
Values may be sent and summed in bfloat16 or wider, within the bound.
A program may use at most 128 MiB of HBM per device.

v0:
```python
import jax
import jax.numpy as jnp
from jax import lax
from jax.sharding import PartitionSpec as P

EDGE = 16
QUANT = 1024


batch_blocks = 4


def spline(offset):
    magnitude = jnp.abs(offset)
    inner_part = 0.75 - magnitude * magnitude
    outer_part = 0.5 * (1.5 - magnitude) * (1.5 - magnitude)
    return jnp.where(magnitude < 0.5, inner_part, jnp.where(magnitude < 1.5, outer_part, 0.0))


def particle_table(
    particle_mass, particle_velocity, particle_affine, particle_cell, particle_fraction, block_count
):
    blocks = block_count.shape[0]
    batch_shape = (blocks, particle_mass.shape[0] // blocks)
    places = jnp.arange(batch_shape[1], dtype=jnp.int32)
    present = places[None, :] < block_count[:, None]
    live_mass = jnp.where(present, particle_mass.reshape(batch_shape), 0.0)
    position = (
        particle_cell.astype(jnp.float32)
        + 0.5
        + (particle_fraction.astype(jnp.float32) + 0.5) / QUANT
    )
    return jnp.concatenate(
        [
            live_mass[None],
            particle_velocity.reshape((3,) + batch_shape),
            particle_affine.reshape((9,) + batch_shape),
            position.reshape((3,) + batch_shape),
        ],
        axis=0,
    )


def stencil(particle_data):
    node_coords = jnp.arange(EDGE, dtype=jnp.float32)
    offset = node_coords[None, :, None, None] - particle_data[13:16][:, None]
    weights = spline(offset)
    return (weights, weights * offset)


def planes(weights, slopes):

    def outer(first_factor, second_factor):
        product_table = first_factor[:, None] * second_factor[None, :]
        return product_table.reshape((EDGE * EDGE,) + product_table.shape[2:]).astype(jnp.bfloat16)

    return (
        outer(weights[1], weights[2]),
        outer(slopes[1], weights[2]),
        outer(weights[1], slopes[2]),
    )


def deposit(particle_data):
    batch_shape = particle_data.shape[1:]
    weights, slopes = stencil(particle_data)
    plane_zero, plane_one, plane_two = planes(weights, slopes)
    live_mass = particle_data[0]
    along_x = weights[0]
    slope_x = slopes[0]
    affine = particle_data[4:13].reshape((3, 3) + batch_shape)
    mass_lead = (live_mass[None] * along_x)[None]
    momentum_lead = live_mass[None, None] * (
        particle_data[1:4][:, None] * along_x[None] + affine[:, 0][:, None] * slope_x[None]
    )
    lead_zero = jnp.concatenate([mass_lead, momentum_lead], axis=0).astype(jnp.bfloat16)
    lead_one = (live_mass[None, None] * affine[:, 1][:, None] * along_x[None]).astype(jnp.bfloat16)
    lead_two = (live_mass[None, None] * affine[:, 2][:, None] * along_x[None]).astype(jnp.bfloat16)

    def contract(lead, plane):
        flattened = lead.reshape((-1,) + batch_shape)
        return jnp.einsum("anp,bnp->nab", flattened, plane, preferred_element_type=jnp.float32)

    count_blocks = batch_shape[0]
    dep_zero = contract(lead_zero, plane_zero).reshape(count_blocks, 4, -1)
    dep_one = contract(lead_one, plane_one).reshape(count_blocks, 3, -1)
    dep_two = contract(lead_two, plane_two).reshape(count_blocks, 3, -1)
    return jnp.concatenate([dep_zero[:, :1], dep_zero[:, 1:] + dep_one + dep_two], axis=1)


def interpolate(particle_data, grid_rows):
    batch_shape = particle_data.shape[1:]
    weights, slopes = stencil(particle_data)
    plane_zero, plane_one, plane_two = planes(weights, slopes)
    along_x = weights[0]
    slope_x = slopes[0]
    flattened = grid_rows.reshape(batch_shape[0], 3 * EDGE, EDGE * EDGE)

    def contract(plane):
        moment = jnp.einsum("nab,bnp->anp", flattened, plane, preferred_element_type=jnp.float32)
        return moment.reshape((3, EDGE) + batch_shape)

    moment_zero = contract(plane_zero)
    moment_one = contract(plane_one)
    moment_two = contract(plane_two)
    velocity_out = jnp.sum(along_x[None] * moment_zero, axis=1)
    column_zero = 4.0 * jnp.sum(slope_x[None] * moment_zero, axis=1)
    column_one = 4.0 * jnp.sum(along_x[None] * moment_one, axis=1)
    column_two = 4.0 * jnp.sum(along_x[None] * moment_two, axis=1)
    affine_out = jnp.stack([column_zero, column_one, column_two], axis=1).reshape(
        (9,) + batch_shape
    )
    present = (particle_data[0] > 0.0).astype(jnp.float32)
    return jnp.concatenate([velocity_out, affine_out], axis=0) * present[None]


def deposit_all(particle_data):
    block_total = particle_data.shape[1]

    def deposit_advance(state_carry, step_index):
        portion = lax.dynamic_slice_in_dim(
            particle_data, step_index * batch_blocks, batch_blocks, 1
        )
        return (state_carry, deposit(portion))

    unused, stacked = lax.scan(
        deposit_advance,
        jnp.zeros((), jnp.float32),
        jnp.arange(block_total // batch_blocks, dtype=jnp.int32),
    )
    return stacked.reshape((block_total,) + stacked.shape[2:])


def interpolate_all(particle_data, grid_rows):
    block_total = particle_data.shape[1]

    def interpolate_advance(step_index, result):
        first_block = step_index * batch_blocks
        portion = lax.dynamic_slice_in_dim(particle_data, first_block, batch_blocks, 1)
        cell_rows = lax.dynamic_slice_in_dim(grid_rows, first_block, batch_blocks, 0)
        return lax.dynamic_update_slice_in_dim(
            result, interpolate(portion, cell_rows), first_block, 1
        )

    initial = jnp.zeros((12, block_total, particle_data.shape[2]), jnp.float32)
    return lax.fori_loop(0, block_total // batch_blocks, interpolate_advance, initial)


def send_slots(owners, group_size, capacity):
    targets = jnp.arange(group_size, dtype=jnp.int32)
    matches = (owners[:, None] == targets[None, :]).astype(jnp.int32)
    earlier = jnp.cumsum(matches, axis=0) - matches
    ranking = jnp.sum(earlier * matches, axis=1)
    return owners * capacity + ranking


def slot_sources(destination, slot_count):
    positions = jnp.arange(slot_count, dtype=jnp.int32)
    matches = destination[None, :] == positions[:, None]
    block_numbers = jnp.arange(destination.shape[0], dtype=jnp.int32)
    source = jnp.sum(jnp.where(matches, block_numbers[None, :], 0), axis=1)
    return (source, jnp.any(matches, axis=1))


def match_tiles(arrived_tiles, tile_count):
    tile_numbers = jnp.arange(tile_count, dtype=jnp.float32)
    return (arrived_tiles[None, :] == tile_numbers[:, None]).astype(jnp.float32)


def update_grid(deposits, tile_match, cell_drag):
    tile_count = tile_match.shape[0]
    flattened = deposits.reshape(deposits.shape[0], -1)
    summed = jnp.dot(
        tile_match, flattened, precision=lax.Precision.HIGHEST, preferred_element_type=jnp.float32
    )
    summed = summed.reshape((tile_count,) + deposits.shape[1:])
    grid_velocity = summed[:, 1:] / (summed[:, :1] + cell_drag[:, None, :])
    rounded = grid_velocity.astype(jnp.bfloat16)
    picked = jnp.dot(
        tile_match.T.astype(jnp.bfloat16),
        rounded.reshape(tile_count, -1),
        preferred_element_type=jnp.float32,
    )
    cell_rows = picked.astype(jnp.bfloat16).reshape((deposits.shape[0], 3, -1))
    return (grid_velocity, cell_rows)


def per_device(
    particle_mass,
    particle_velocity,
    particle_affine,
    particle_cell,
    particle_fraction,
    block_owner,
    block_slot,
    block_count,
    cell_drag,
):
    group_size = lax.axis_size(("gy", "gz"))
    blocks = block_count.shape[0]
    capacity = max(1, 2 * blocks // group_size)
    slot_count = group_size * capacity
    tile_count = cell_drag.shape[0]
    particle_data = particle_table(
        particle_mass,
        particle_velocity,
        particle_affine,
        particle_cell,
        particle_fraction,
        block_count,
    )
    destination = send_slots(block_owner[:, 0], group_size, capacity)
    source, filled = slot_sources(destination, slot_count)
    tile_ids = jnp.where(filled, jnp.take(block_slot, source), -1).astype(jnp.float32)
    deposits = deposit_all(particle_data)
    outgoing = jnp.where(filled[:, None, None], jnp.take(deposits, source, axis=0), 0.0)
    arrived, arrived_tiles = (
        lax.all_to_all(outgoing, ("gy", "gz"), split_axis=0, concat_axis=0, tiled=True),
        lax.all_to_all(tile_ids, ("gy", "gz"), split_axis=0, concat_axis=0, tiled=True),
    )
    tile_match = match_tiles(arrived_tiles, tile_count)
    grid_velocity, cell_rows = update_grid(arrived, tile_match, cell_drag)
    returned = lax.all_to_all(cell_rows, ("gy", "gz"), split_axis=0, concat_axis=0, tiled=True)
    finished = interpolate_all(particle_data, jnp.take(returned, destination, axis=0))
    new_velocity = finished[:3].reshape(3, -1)
    new_affine = finished[3:].reshape(9, -1)
    return (grid_velocity, new_velocity, new_affine)


def solution(mesh):
    return jax.shard_map(
        per_device,
        mesh=mesh,
        in_specs=(
            P(("gx", "gy", "gz")),
            P(None, ("gx", "gy", "gz")),
            P(None, ("gx", "gy", "gz")),
            P(None, ("gx", "gy", "gz")),
            P(None, ("gx", "gy", "gz")),
            P(("gx", "gy", "gz"), None),
            P(("gx", "gy", "gz")),
            P(("gx", "gy", "gz")),
            P(("gx", "gy", "gz"), None),
        ),
        out_specs=(
            P(("gx", "gy", "gz"), None, None),
            P(None, ("gx", "gy", "gz")),
            P(None, ("gx", "gy", "gz")),
        ),
        check_vma=False,
    )
```

profile of v0, /device:TPU:13, one launch (start us, length us, event | category | flops | bytes accessed | tf_op | source)
XLA Modules:
  0.0 659.1 jit_solution(10529736568579550010)
XLA Ops:
  5.6 6.5 all-to-all-start
  12.2 2.8 copy.92
  18.4 167.9 %while.23 = (s32[]{:T(128)}, f32[16,4,4,4096]{3,2,1,0:T(4,128)}, s32[16]{0:T(128)S(1)}, f32[16,64,512]{2,1,0:T(8,128)}, s32[]{:T(128)}, /*index=5*/s32[]{:T(128)...) while((s32[]{:T(128)}, f32[16,4,4,4096]{3,2,1,0:T(4,128)}, s32[16]{0:T(128)S(1)}, ...), condition=%wide.region_5.6_spmd, body=%wide.region_4.5_spmd.sunk | while | flops 173355008 | bytes 15483619 | solution.py:126
  186.2 11.4 %gather_fusion.1 = f32[128,4,4096]{2,1,0:T(4,128)} fusion(f32[64,4,4096]{2,1,0:T(4,128)} %bitcast.211, s32[1024]{0:T(1024)S(1)} %pad_clamp_fusion.1), kind=kCustom, calls=%fused_computation.1 | custom fusion | bytes 16777728 | tf_op jit(solution)/shard_map/jit(_take)/gather | solution.py:216
  197.7 11.6 %select_select_fusion = f32[128,4,4096]{2,1,0:T(4,128)} fusion(f32[128,4,4096]{2,1,0:T(4,128)} %gather_fusion.1, pred[128]{0:T(512)(128)(4,1)S(1)} %compare_and_fusion, pred[128]{0:T(512)(128)(4,1)S(1)} %fusion.22), kind=kLoop, calls=%fused_computation.72 | loop fusion | flops 4194304 | bytes 16777472 | tf_op jit(solution)/shard_map/jit(_where)/select_n | solution.py:216
  209.3 6.0 all-to-all-start.1
  216.6 181.1 %all-to-all-done.1 = f32[128,4,4096]{2,1,0:T(4,128)} async-done(((f32[128,4,4096]{2,1,0:T(4,128)}), f32[128,4,4096]{2,1,0:T(4,128)}, u32[]{:S(2)}, u32[]{:S(2)}) %all-to-all-start.1) | async-done | bytes 8388640 | tf_op jit(solution)/shard_map/all_to_all | solution.py:218
  397.7 10.0 %copy.86 = f32[128,4,4096]{0,2,1:T(8,128)} copy(f32[128,4,4096]{2,1,0:T(4,128)} %all-to-all-done.1) | data formatting | bytes 16777216 | tf_op jit(solution)/shard_map/all_to_all | solution.py:218
  407.7 8.1 %fusion.17 = f32[32,4,4096]{2,0,1:T(8,128)S(1)} fusion(f32[128,4,4096]{0,2,1:T(8,128)} %copy.86, f32[128]{0:T(128)S(1)} %eq.54), kind=kOutput, calls=%fused_computation.70 | convolution fusion | flops 805310464 | bytes 10486272 | tf_op jit(solution)/shard_map/dot_general | solution.py:173
  417.3 2.7 convolution_convert_fusion
  420.0 3.5 copy.88
  423.4 5.5 copy.89
  429.0 4.9 all-to-all-start.2
  433.9 92.4 %all-to-all-done.2 = bf16[128,3,4096]{2,1,0:T(4,128)(2,1)} async-done(((bf16[128,3,4096]{2,1,0:T(4,128)(2,1)}), bf16[128,3,4096]{2,1,0:T(4,128)(2,1)}, u32[]{:S(2)}, u32[]{:S(2)}) %all-to-all-start.2) | async-done | bytes 3145760 | tf_op jit(solution)/shard_map/all_to_all | solution.py:223
  526.3 4.5 gather_fusion.2
  530.9 2.4 broadcast_select_fusion
  534.6 118.2 %while.24 = (s32[]{:T(128)}, f32[12,64,512]{2,1,0:T(8,128)}, f32[16,64,512]{2,1,0:T(8,128)}, bf16[64,3,4096]{2,1,0:T(4,128)(2,1)}, s32[]{:T(128)}, /*index=5*/s32[]{:T(128)}, s32[]{:T(128)}, s32[]{:T(128)}, s32[]{}) while((s32[]{:T(128)}, f32[12,64,512]{2,1,0:T(8,128)}, f32[16,64,512]{2,1,0:T(8,128)}, bf16[64,3,4096]{2,1,0:T(4,128)(2,1)}, ...), condition=%wide.region_11.12_spmd, body=%wide.region_6.11_spmd.sunk | while | flops 156190720 | bytes 13369515 | solution.py:146
  536.6 1.6 constant_dynamic-slice_fusion.11
  544.0 1.6 constant_dynamic-slice_fusion.11
  551.3 1.6 constant_dynamic-slice_fusion.11
  558.7 1.6 constant_dynamic-slice_fusion.11
  566.1 1.6 constant_dynamic-slice_fusion.11
  573.5 1.6 constant_dynamic-slice_fusion.11
  580.9 1.6 constant_dynamic-slice_fusion.11
  588.2 1.6 constant_dynamic-slice_fusion.11
  595.6 1.6 constant_dynamic-slice_fusion.11
  603.0 1.6 constant_dynamic-slice_fusion.11
  610.4 1.6 constant_dynamic-slice_fusion.11
  617.8 1.6 constant_dynamic-slice_fusion.11
  625.2 1.6 constant_dynamic-slice_fusion.11
  632.6 1.6 constant_dynamic-slice_fusion.11
  655.5 2.5 copy.95
  (732 shorter events, 265.7 us)
Async XLA Ops:
  0.6 2.7 copy-start
  5.6 203.7 %all-to-all-start = ((f32[16,8,1]{1,2,0:T(1,128)}), f32[16,8,1]{1,2,0:T(1,128)S(1)}, u32[]{:S(2)}, u32[]{:S(2)}) async-start(f32[16,8,1]{1,2,0:T(1,128)} %copy.85), calls=%async_computation | async-start | bytes 16384 | tf_op jit(solution)/shard_map/all_to_all | solution.py:219
  15.0 0.9 copy-start.6
  15.0 1.1 copy-start.2
  15.0 1.3 copy-start.3
  15.0 1.5 copy-start.4
  15.9 0.8 copy-start.8
  209.3 188.3 %all-to-all-start.1 = ((f32[128,4,4096]{2,1,0:T(4,128)}), f32[128,4,4096]{2,1,0:T(4,128)}, u32[]{:S(2)}, u32[]{:S(2)}) async-start(f32[128,4,4096]{2,1,0:T(4,128)} %select_select_fusion), calls=%async_computation.1 | async-start | bytes 16777216 | tf_op jit(solution)/shard_map/all_to_all | solution.py:218
  407.7 8.1 %copy-start.5 = (f32[32,4096]{1,0:T(8,128)S(1)}, f32[32,4096]{1,0:T(8,128)}, u32[]{:S(2)}) copy-start(f32[32,4096]{1,0:T(8,128)} %param.21) | copy-start | bytes 1572868
  429.0 4.9 copy-start.7
  429.0 97.4 %all-to-all-start.2 = ((bf16[128,3,4096]{2,1,0:T(4,128)(2,1)}), bf16[128,3,4096]{2,1,0:T(4,128)(2,1)}, u32[]{:S(2)}, u32[]{:S(2)}) async-start(bf16[128,3,4096]{2,1,0:T(4,128)(2,1)} %copy.89), calls=%async_computation.2 | async-start | bytes 8388608 | tf_op jit(solution)/shard_map/all_to_all | solution.py:223
  655.5 3.6 copy-start.1
where the time goes:
time: 665 us; the launch traced here: 659 us
  waiting for transfers between devices  274 us (41%)
  local copies, waits for them, and re-layouts  164 us (25%)
  other arithmetic  114 us (17%)
  matrix products  74.8 us (11%)
  starting transfers between devices  17.4 us (3%)
  loops' own time  13.9 us (2%)
    all_to_all x1, waiting for transfers between devices, per_device(): lax.all_to_all(outgoing, ('gy', 'gz'), split_axis=0, concat_axis=0, tiled...  181 us
    all_to_all x1, waiting for transfers between devices, per_device(): lax.all_to_all(cell_rows, ('gy', 'gz'), split_axis=0, concat_axis=0, tile...  92.4 us
    dot_general x48, matrix products, contract(): jnp.einsum('anp,bnp->nab', flattened, plane, preferred_element_type=jnp.f...  50.1 us
    convert_element_type x32, other arithmetic, outer(): product_table.reshape((EDGE * EDGE,) + product_table.shape[2:])  29 us
    dynamic_slice x16, local copies, waits for them, and re-layouts, interpolate_advance(): lax.dynamic_slice_in_dim(grid_rows, first_block, batch_blocks, 0)  25.8 us
    reshape x16, local copies, waits for them, and re-layouts, interpolate(): flattened = grid_rows.reshape(batch_shape[0], 3 * EDGE, EDGE * EDGE)  16.8 us
    slice x16, local copies, waits for them, and re-layouts, deposit(): affine = particle_data[4:13].reshape((3, 3) + batch_shape)  14.9 us
    another operation x32, other arithmetic  14.9 us
  transfers between devices with their start and end apart: 3, of which 2 were waited for; matrix products, arithmetic and copies ran while one was open for 28% of the time, Pallas kernels for 0%

commit v1 on v0

v1 whole, which is shorter than its diff:
```python
import functools

import jax
import jax.numpy as jnp
from jax import lax
from jax.experimental import pallas as pl
from jax.experimental.pallas import tpu as pltpu
from jax.sharding import PartitionSpec as P

EDGE = 16
QUANT = 1024
LANES = 128
FIELDS = 20
RESULTS = 12
UNROLL = 2
GROUP_AXES = ("gy", "gz")
F32 = jnp.float32
BF16 = jnp.bfloat16


def pack_kernel(
    capacity,
    owner_ref,
    slot_ref,
    count_ref,
    mass_ref,
    velocity_ref,
    affine_ref,
    cell_ref,
    fraction_ref,
    payload_ref,
    tiles_ref,
    dest_ref,
    used_ref,
    stage_ref,
):
    blocks = owner_ref.shape[0]
    slots = payload_ref.shape[0]
    width = mass_ref.shape[1]

    def clear_used(i, carry):
        used_ref[i] = 0
        return carry

    lax.fori_loop(0, used_ref.shape[0], clear_used, 0)

    def clear_tiles(i, carry):
        tiles_ref[i] = -1
        return carry

    lax.fori_loop(0, slots, clear_tiles, 0)

    lane = lax.broadcasted_iota(jnp.int32, (1, width), 1)

    def pack(block, carry):
        owner = owner_ref[block]
        rank = used_ref[owner]
        used_ref[owner] = rank + 1
        where = owner * capacity + rank
        dest_ref[block] = where
        tiles_ref[where] = slot_ref[block]
        cols = pl.ds(pl.multiple_of(block * width, LANES), width)
        live = jnp.where(lane < count_ref[block], mass_ref[pl.ds(block, 1), :], 0.0)
        velocity = velocity_ref[:, cols]
        affine = affine_ref[:, cols]
        code = cell_ref[:, cols] * QUANT + fraction_ref[:, cols]
        high = (code >> 7).astype(F32)
        low = (code & 127).astype(F32)
        for q in range(width // LANES):
            part = slice(q * LANES, (q + 1) * LANES)
            base = q * FIELDS
            stage_ref[base : base + 1] = live[:, part]
            stage_ref[base + 1 : base + 4] = velocity[:, part]
            stage_ref[base + 4 : base + 13] = affine[:, part]
            stage_ref[base + 13 : base + 16] = high[:, part]
            stage_ref[base + 16 : base + 19] = low[:, part]
        payload_ref[where] = stage_ref[...].astype(BF16)
        return carry

    lax.fori_loop(0, blocks, pack, 0)


def pack(capacity, slots, group_size, owner, slot, count, mass, velocity, affine, cell, fraction):
    blocks = owner.shape[0]
    width = mass.shape[0] // blocks
    rows = width // LANES * FIELDS
    smem = pl.BlockSpec(memory_space=pltpu.SMEM)
    vmem = pl.BlockSpec(memory_space=pltpu.VMEM)
    return pl.pallas_call(
        functools.partial(pack_kernel, capacity),
        name="pack",
        out_shape=(
            jax.ShapeDtypeStruct((slots, rows, LANES), BF16),
            jax.ShapeDtypeStruct((slots,), jnp.int32),
            jax.ShapeDtypeStruct((blocks,), jnp.int32),
        ),
        in_specs=[smem] * 3 + [vmem] * 5,
        out_specs=(vmem, smem, smem),
        scratch_shapes=[pltpu.SMEM((group_size,), jnp.int32), pltpu.VMEM((rows, LANES), F32)],
        compiler_params=pltpu.CompilerParams(vmem_limit_bytes=48 << 20),
    )(owner, slot, count, mass.reshape(blocks, width), velocity, affine, cell, fraction)


def spread(rows, field):
    quarters = rows.shape[0] // FIELDS
    return jnp.concatenate(
        [
            jnp.broadcast_to(rows[q * FIELDS + field : q * FIELDS + field + 1], (EDGE, LANES))
            for q in range(quarters)
        ],
        axis=1,
    )


def stencil(rows, node, dim):
    position = (
        spread(rows, 13 + dim) * (128.0 / QUANT)
        + spread(rows, 16 + dim) * (1.0 / QUANT)
        + (0.5 + 0.5 / QUANT)
    )
    offset = node - position
    magnitude = jnp.abs(offset)
    outer_part = jnp.maximum(1.5 - magnitude, 0.0)
    weight = jnp.where(
        magnitude < 0.5, 0.75 - magnitude * magnitude, 0.5 * outer_part * outer_part
    )
    return weight, weight * offset


def outer(first, second):
    table = first[:, None, :] * second[None, :, :]
    return table.reshape(EDGE * EDGE, first.shape[1])


def planes(rows, node):
    weight_y, slope_y = stencil(rows, node, 1)
    weight_z, slope_z = stencil(rows, node, 2)
    weight_y, slope_y = weight_y.astype(BF16), slope_y.astype(BF16)
    weight_z, slope_z = weight_z.astype(BF16), slope_z.astype(BF16)
    return outer(weight_y, weight_z), outer(slope_y, weight_z), outer(weight_y, slope_z)


def contract(lead, plane):
    return lax.dot_general(lead, plane, (((1,), (1,)), ((), ())), preferred_element_type=F32)


def deposit(rows):
    width = rows.shape[0] // FIELDS * LANES
    node = lax.broadcasted_iota(jnp.int32, (EDGE, width), 0).astype(F32)
    weight_x, slope_x = stencil(rows, node, 0)
    plane_zero, plane_one, plane_two = planes(rows, node)
    mass_x = spread(rows, 0) * weight_x
    mass_slope = spread(rows, 0) * slope_x
    lead_zero, lead_one, lead_two = [mass_x], [], []
    for d in range(3):
        lead_zero.append(spread(rows, 1 + d) * mass_x + spread(rows, 4 + 3 * d) * mass_slope)
        lead_one.append(spread(rows, 5 + 3 * d) * mass_x)
        lead_two.append(spread(rows, 6 + 3 * d) * mass_x)
    lead_zero, lead_one, lead_two = [
        jnp.concatenate([part.astype(BF16) for part in lead], axis=0)
        for lead in (lead_zero, lead_one, lead_two)
    ]
    first = contract(lead_zero, plane_zero)
    rest = contract(lead_one, plane_one) + contract(lead_two, plane_two)
    return first[:EDGE], first[EDGE:] + rest


def interpolate(rows, grid_rows):
    width = rows.shape[0] // FIELDS * LANES
    node = lax.broadcasted_iota(jnp.int32, (EDGE, width), 0).astype(F32)
    weight_x, slope_x = stencil(rows, node, 0)
    moment_zero, moment_one, moment_two = [
        jnp.dot(grid_rows, plane, preferred_element_type=F32) for plane in planes(rows, node)
    ]
    slope_x = 4.0 * slope_x
    weight_four = 4.0 * weight_x
    velocity, affine = [], []
    for d in range(3):
        part = slice(d * EDGE, (d + 1) * EDGE)

        def total(factor, moment):
            return jnp.sum(factor * moment[part], axis=0, keepdims=True)

        velocity.append(total(weight_x, moment_zero))
        affine.append(total(slope_x, moment_zero))
        affine.append(total(weight_four, moment_one))
        affine.append(total(weight_four, moment_two))
    return velocity + affine


def grid_kernel(
    tiles_ref, arrived_ref, drag_ref, grid_ref, out_ref, order_ref, sums_ref, round_ref, stage_ref
):
    slots = arrived_ref.shape[0]
    tile_count = drag_ref.shape[0]
    plane_size = EDGE * EDGE

    def collect(s, filled):
        order_ref[filled] = s
        return filled + (tiles_ref[s] >= 0).astype(jnp.int32)

    order_ref[0] = 0
    filled = lax.fori_loop(0, slots, collect, 0)
    last = order_ref[jnp.maximum(filled - 1, 0)]
    for u in range(UNROLL):
        order_ref[filled + u] = last

    def start(t, carry):
        for x in range(EDGE):
            sums_ref[t, x : x + 1, :] = drag_ref[
                pl.ds(t, 1), x * plane_size : (x + 1) * plane_size
            ]
        sums_ref[t, EDGE:, :] = jnp.zeros((3 * EDGE, plane_size), F32)
        return carry

    lax.fori_loop(0, tile_count, start, 0)
    steps = (filled + UNROLL - 1) // UNROLL

    def scatter(step, carry):
        results = []
        for u in range(UNROLL):
            at = step * UNROLL + u
            s = order_ref[at]
            results.append(
                (
                    jnp.where(at < filled, tiles_ref[s], tile_count),
                    deposit(arrived_ref[s].astype(F32)),
                )
            )
        for tile, (mass, momentum) in results:
            sums_ref[tile, :EDGE, :] += mass
            sums_ref[tile, EDGE:, :] += momentum
        return carry

    lax.fori_loop(0, steps, scatter, 0)

    def divide(t, carry):
        mass = sums_ref[t, :EDGE, :]
        parts = [
            sums_ref[t, (d + 1) * EDGE : (d + 2) * EDGE, :] / mass for d in range(3)
        ]
        velocity = jnp.concatenate(parts, axis=0)
        round_ref[t] = velocity.astype(BF16)
        for d in range(3):
            for x in range(EDGE):
                grid_ref[t, d : d + 1, x * plane_size : (x + 1) * plane_size] = parts[d][
                    x : x + 1
                ]
        return carry

    lax.fori_loop(0, tile_count, divide, 0)

    def gather(step, carry):
        for u in range(UNROLL):
            s = order_ref[step * UNROLL + u]
            results = interpolate(arrived_ref[s].astype(F32), round_ref[tiles_ref[s]])
            quarters = results[0].shape[1] // LANES
            for a in range(RESULTS):
                for q in range(quarters):
                    row = q * RESULTS + a
                    stage_ref[u, row : row + 1] = results[a][:, q * LANES : (q + 1) * LANES]
            out_ref[s] = stage_ref[u].astype(BF16)
        return carry

    lax.fori_loop(0, steps, gather, 0)


def grid_step(tiles, arrived, drag):
    slots, rows, _ = arrived.shape
    out_rows = rows // FIELDS * RESULTS
    tile_count, cells = drag.shape
    plane_size = EDGE * EDGE
    smem = pl.BlockSpec(memory_space=pltpu.SMEM)
    vmem = pl.BlockSpec(memory_space=pltpu.VMEM)
    return pl.pallas_call(
        grid_kernel,
        name="grid_step",
        out_shape=(
            jax.ShapeDtypeStruct((tile_count, 3, cells), F32),
            jax.ShapeDtypeStruct((slots, out_rows, LANES), BF16),
        ),
        in_specs=[smem, vmem, vmem],
        out_specs=(vmem, vmem),
        scratch_shapes=[
            pltpu.SMEM((slots + UNROLL,), jnp.int32),
            pltpu.VMEM((tile_count + 1, 4 * EDGE, plane_size), F32),
            pltpu.VMEM((tile_count, 3 * EDGE, plane_size), BF16),
            pltpu.VMEM((UNROLL, out_rows, LANES), F32),
        ],
        compiler_params=pltpu.CompilerParams(vmem_limit_bytes=48 << 20),
    )(tiles, arrived, drag)


def unpack_kernel(dest_ref, count_ref, returned_ref, velocity_ref, affine_ref):
    blocks = dest_ref.shape[0]
    width = velocity_ref.shape[1] // blocks
    lane = lax.broadcasted_iota(jnp.int32, (1, LANES), 1)

    def unpack(block, carry):
        rows = returned_ref[dest_ref[block]].astype(F32)
        for q in range(width // LANES):
            present = lane + q * LANES < count_ref[block]
            cols = pl.ds(pl.multiple_of(block * width + q * LANES, LANES), LANES)
            part = jnp.where(present, rows[q * RESULTS : (q + 1) * RESULTS], 0.0)
            velocity_ref[:, cols] = part[:3]
            affine_ref[:, cols] = part[3:]
        return carry

    lax.fori_loop(0, blocks, unpack, 0)


def unpack(dest, count, returned, width):
    particles = dest.shape[0] * width
    smem = pl.BlockSpec(memory_space=pltpu.SMEM)
    vmem = pl.BlockSpec(memory_space=pltpu.VMEM)
    return pl.pallas_call(
        unpack_kernel,
        name="unpack",
        out_shape=(
            jax.ShapeDtypeStruct((3, particles), F32),
            jax.ShapeDtypeStruct((9, particles), F32),
        ),
        in_specs=[smem, smem, vmem],
        out_specs=(vmem, vmem),
        compiler_params=pltpu.CompilerParams(vmem_limit_bytes=48 << 20),
    )(dest, count, returned)


def exchange(value):
    return lax.all_to_all(value, GROUP_AXES, split_axis=0, concat_axis=0, tiled=True)


def per_device(
    particle_mass,
    particle_velocity,
    particle_affine,
    particle_cell,
    particle_fraction,
    block_owner,
    block_slot,
    block_count,
    cell_drag,
):
    group_size = lax.axis_size(GROUP_AXES)
    blocks = block_count.shape[0]
    capacity = max(1, 2 * blocks // group_size)
    slots = group_size * capacity
    payload, tiles, dest = pack(
        capacity,
        slots,
        group_size,
        block_owner[:, 0],
        block_slot,
        block_count,
        particle_mass,
        particle_velocity,
        particle_affine,
        particle_cell,
        particle_fraction,
    )
    arrived_tiles = exchange(tiles)
    arrived = exchange(payload)
    grid_velocity, results = grid_step(arrived_tiles, arrived, cell_drag)
    returned = exchange(results)
    new_velocity, new_affine = unpack(
        dest, block_count, returned, particle_mass.shape[0] // blocks
    )
    return grid_velocity, new_velocity, new_affine


def solution(mesh):
    everywhere = ("gx", "gy", "gz")
    return jax.shard_map(
        per_device,
        mesh=mesh,
        in_specs=(
            P(everywhere),
            P(None, everywhere),
            P(None, everywhere),
            P(None, everywhere),
            P(None, everywhere),
            P(everywhere, None),
            P(everywhere),
            P(everywhere),
            P(everywhere, None),
        ),
        out_specs=(P(everywhere, None, None), P(None, everywhere), P(None, everywhere)),
        check_vma=False,
    )
```

time: 665 us -> 213 us (0.32); the launches traced: 659 us -> 215 us
  waiting for transfers between devices: 274 us -> 90 us
  local copies, waits for them, and re-layouts: 164 us -> 13.3 us
  other arithmetic: 114 us -> 0.67 us
  matrix products: 74.8 us -> 0 us
  Pallas kernels: 0 us -> 52.9 us
  starting transfers between devices: 17.4 us -> 47.5 us
  loops' own time: 13.9 us -> 0 us
  blocking collectives: 0 us -> 10.2 us
    all_to_all x3 -> x2, waiting for transfers between devices: 274 us -> 90 us  [exchange(): lax.all_to_all(value, GROUP_AXES, split_axis=0, concat_axis=0, tiled=True)]
    dot_general x98 -> x0, matrix products: 74.8 us -> none  [the longest x48 50.1 us: contract(): jnp.einsum('anp,bnp->nab', flattened, plane, preferred_element_type=jnp.f...]
    pallas_call x0 -> x3, Pallas kernels: none -> 52.9 us  [the longest x1 45.6 us: grid_step(): pl.pallas_call(grid_kernel, name='grid_step', out_shape=(jax.ShapeDtypeSt...]
    slice x97 -> x0, local copies, waits for them, and re-layouts: 43.9 us -> none  [the longest x16 14.9 us: deposit(): affine = particle_data[4:13].reshape((3, 3) + batch_shape)]
    dynamic_slice x32 -> x0, local copies, waits for them, and re-layouts: 35.1 us -> none  [the longest x16 25.8 us: interpolate_advance(): lax.dynamic_slice_in_dim(grid_rows, first_block, batch_blocks, 0)]
    all_to_all x3 -> x2, starting transfers between devices: 17.4 us -> 47.5 us  [exchange(): lax.all_to_all(value, GROUP_AXES, split_axis=0, concat_axis=0, tiled=True)]
    convert_element_type x34 -> x0, other arithmetic: 29.8 us -> none  [the longest x32 29 us: outer(): product_table.reshape((EDGE * EDGE,) + product_table.shape[2:])]
    reshape x69 -> x1, local copies, waits for them, and re-layouts: 28.2 us -> 0.93 us  [pack(): mass.reshape(blocks, width)]
  transfers between devices with their start and end apart: 3 -> 2, of which waited for: 2 -> 2; matrix products, arithmetic and copies ran while one was open for 28% -> 2% of each run, Pallas kernels for 0% -> 0%
where the time goes in v1:
time: 213 us; the launch traced here: 215 us
  waiting for transfers between devices  90 us (42%)
  Pallas kernels  52.9 us (25%)
  starting transfers between devices  47.5 us (22%)
  local copies, waits for them, and re-layouts  13.3 us (6%)
  blocking collectives  10.2 us (5%)
    all_to_all x2, waiting for transfers between devices, exchange(): lax.all_to_all(value, GROUP_AXES, split_axis=0, concat_axis=0, tiled=True)  90 us
    all_to_all x2, starting transfers between devices, exchange(): lax.all_to_all(value, GROUP_AXES, split_axis=0, concat_axis=0, tiled=True)  47.5 us
    pallas_call x1, Pallas kernels, grid_step(): pl.pallas_call(grid_kernel, name='grid_step', out_shape=(jax.ShapeDtypeSt...  45.6 us
    unnamed x21, local copies, waits for them, and re-layouts  11.7 us
    all_to_all x1, blocking collectives, exchange(): lax.all_to_all(value, GROUP_AXES, split_axis=0, concat_axis=0, tiled=True)  10.2 us
    pallas_call x1, Pallas kernels, pack(): pl.pallas_call(functools.partial(pack_kernel, capacity), name='pack', out...  4.28 us
  transfers between devices with their start and end apart: 2, of which 2 were waited for; matrix products, arithmetic and copies ran while one was open for 2% of the time, Pallas kernels for 0%

profile of v1, /device:TPU:13, one launch (start us, length us, event | category | flops | bytes accessed | tf_op | source)
XLA Modules:
  0.0 215.1 jit_solution(15943314606144175532)
XLA Ops:
  0.6 0.9 reshape.11.mass_ref
  1.6 0.0 copy-start.1
  1.6 1.6 copy-done.1
  3.2 0.0 copy-start.2
  3.2 1.0 copy-done.2
  4.2 1.0 copy-done.3
  5.2 0.0 copy-start.4
  5.2 1.0 copy-done.4
  6.3 0.0 copy-start.6
  6.3 0.7 copy-done.6
  6.9 0.7 copy-done.8
  7.6 0.0 copy-start.9
  7.6 0.7 copy-done.9
  8.2 4.3 %pack.1 = (bf16[128,80,128]{2,1,0:T(8,128)(2,1)}, s32[128]{0:T(128)S(1)}, s32[64]{0:T(128)S(1)}) custom-call(s32[64]{0:T(128)S(1)} %bitcast.3, s32[64]{0:T(128)S(1)} %copy-done.9, s32[64]{0:T(128)S(1)} %copy-done.6, f32[64,512]{1,0:T(8,128)S(1)} %reshape.11.mass_ref, f32[3,32768]{1,0:T(4,128)S(1)} %copy-done.2, f32[9,32768]{1,0:T(8,128)S(1)} %copy-done.1, ...), custom_call_target="tpu_custom_call" | custom-call | tf_op jit(solution)/shard_map/pack/pallas_call | solution.py:89
  12.5 0.1 all_to_all.13
  12.6 10.2 %all_to_all.21 = s32[16,8,1]{1,2,0:T(1,128)S(1)} all-to-all(s32[16,8,1]{1,2,0:T(1,128)S(1)} %bitcast.4), channel_id=1, replica_groups=mesh['gx'=2,'gy'=4,'gz'=4] {'gy','gz'}, dimensions={0} | all-to-all | bytes 1024 | tf_op jit(solution)/shard_map/all_to_all | solution.py:330
  22.8 0.0 copy-start.5
  22.8 7.0 %all-to-all-start.1 = ((bf16[128,80,128]{2,1,0:T(8,128)(2,1)}), bf16[128,80,128]{2,1,0:T(8,128)(2,1)}, u32[]{:S(2)}, u32[]{:S(2)}) async-start(bf16[128,80,128]{2,1,0:T(8,128)(2,1)} %get-tuple-element.11), calls=%async_computation.1 | async-start | bytes 5242880 | tf_op jit(solution)/shard_map/all_to_all | solution.py:330
  29.8 0.5 broadcast.3
  30.3 0.7 reduce.3
  31.0 0.1 all_to_all.15.tiles_ref
  31.1 57.5 %all-to-all-done.1.arrived_ref = bf16[128,80,128]{2,1,0:T(8,128)(2,1)} async-done(((bf16[128,80,128]{2,1,0:T(8,128)(2,1)}), bf16[128,80,128]{2,1,0:T(8,128)(2,1)}, u32[]{:S(2)}, u32[]{:S(2)}) %all-to-all-start.1) | async-done | bytes 2621472 | tf_op jit(solution)/shard_map/all_to_all | solution.py:330
  88.6 0.0 copy-done.5
  88.6 45.6 %grid_step.1 = (f32[32,3,4096]{2,1,0:T(4,128)S(1)}, bf16[128,48,128]{2,1,0:T(8,128)(2,1)}) custom-call(s32[128]{0:T(128)S(1)} %all_to_all.15.tiles_ref, bf16[128,80,128]{2,1,0:T(8,128)(2,1)} %all-to-all-done.1.arrived_ref, f32[32,4096]{1,0:T(8,128)S(1)} %copy-done.5), custom_call_target="tpu_custom_call" | custom-call | tf_op jit(solution)/shard_map/grid_step/pallas_call | solution.py:275
  134.2 0.0 copy-start
  134.2 1.3 copy-done
  135.6 40.4 %all-to-all-start.2 = ((bf16[128,48,128]{2,1,0:T(8,128)(2,1)}), bf16[128,48,128]{2,1,0:T(8,128)(2,1)S(1)}, u32[]{:S(2)}, u32[]{:S(2)}) async-start(bf16[128,48,128]{2,1,0:T(8,128)(2,1)} %get-tuple-element.14), calls=%async_computation.2 | async-start | bytes 3145728 | tf_op jit(solution)/shard_map/all_to_all | solution.py:330
  176.0 0.0 copy-start.7
  176.0 3.7 %copy.15 = f32[32,3,4096]{2,0,1:T(8,128)} copy(f32[32,3,4096]{2,1,0:T(4,128)} %copy-done) | data formatting | bytes 3145728
  179.7 32.5 %all-to-all-done.2.returned_ref = bf16[128,48,128]{2,1,0:T(8,128)(2,1)S(1)} async-done(((bf16[128,48,128]{2,1,0:T(8,128)(2,1)}), bf16[128,48,128]{2,1,0:T(8,128)(2,1)S(1)}, u32[]{:S(2)}, u32[]{:S(2)}) %all-to-all-start.2) | async-done | bytes 1572896 | tf_op jit(solution)/shard_map/all_to_all | solution.py:330
  212.2 0.0 copy-done.7
  212.2 2.9 %unpack.1 = (f32[3,32768]{1,0:T(4,128)}, f32[9,32768]{1,0:T(8,128)}) custom-call(s32[64]{0:T(128)S(1)} %get-tuple-element.13.dest_ref, s32[64]{0:T(128)S(1)} %copy-done.7, bf16[128,48,128]{2,1,0:T(8,128)(2,1)S(1)} %all-to-all-done.2.returned_ref), custom_call_target="tpu_custom_call" | custom-call | tf_op jit(solution)/shard_map/unpack/pallas_call | solution.py:316
  (2 shorter events, 0.0 us)
Async XLA Ops:
  1.6 1.6 copy-start.1
  3.2 1.0 copy-start.2
  4.2 1.0 copy-start.3
  5.2 1.0 copy-start.4
  6.3 0.7 copy-start.6
  6.9 0.7 copy-start.8
  7.6 0.7 copy-start.9
  22.8 65.8 %copy-start.5 = (f32[32,4096]{1,0:T(8,128)S(1)}, f32[32,4096]{1,0:T(8,128)}, u32[]{:S(2)}) copy-start(f32[32,4096]{1,0:T(8,128)} %drag_ref.1) | copy-start | bytes 1572868
  22.8 65.8 %all-to-all-start.1 = ((bf16[128,80,128]{2,1,0:T(8,128)(2,1)}), bf16[128,80,128]{2,1,0:T(8,128)(2,1)}, u32[]{:S(2)}, u32[]{:S(2)}) async-start(bf16[128,80,128]{2,1,0:T(8,128)(2,1)} %get-tuple-element.11), calls=%async_computation.1 | async-start | bytes 5242880 | tf_op jit(solution)/shard_map/all_to_all | solution.py:330
  134.2 1.3 copy-start
  135.6 76.6 %all-to-all-start.2 = ((bf16[128,48,128]{2,1,0:T(8,128)(2,1)}), bf16[128,48,128]{2,1,0:T(8,128)(2,1)S(1)}, u32[]{:S(2)}, u32[]{:S(2)}) async-start(bf16[128,48,128]{2,1,0:T(8,128)(2,1)} %get-tuple-element.14), calls=%async_computation.2 | async-start | bytes 3145728 | tf_op jit(solution)/shard_map/all_to_all | solution.py:330
  176.0 36.2 %copy-start.7 = (s32[64]{0:T(128)S(1)}, s32[64]{0:T(128)}, u32[]{:S(2)}) copy-start(s32[64]{0:T(128)} %count_ref.3) | copy-start | bytes 772

commit v2 on v1

v2 whole, which is shorter than its diff:
```python
import functools

import jax
import jax.numpy as jnp
from jax import lax
from jax.experimental import pallas as pl
from jax.experimental.pallas import tpu as pltpu
from jax.sharding import PartitionSpec as P

EDGE = 16
QUANT = 1024
LANES = 128
FIELDS = 20
RESULTS = 12
UNROLL = 4
HALVES = 2
GROUP_AXES = ("gy", "gz")
F32 = jnp.float32
BF16 = jnp.bfloat16


SMEM = pl.BlockSpec(memory_space=pltpu.SMEM)
VMEM = pl.BlockSpec(memory_space=pltpu.VMEM)
PARAMS = pltpu.CompilerParams(vmem_limit_bytes=48 << 20)


def cost(flops):
    return pl.CostEstimate(flops=flops, bytes_accessed=1 << 22, transcendentals=0)


def pack_kernel(
    portion,
    owner_ref,
    slot_ref,
    count_ref,
    mass_ref,
    velocity_ref,
    affine_ref,
    cell_ref,
    fraction_ref,
    *rest,
):
    payload_refs, (dest_ref, used_ref, stage_ref) = rest[:-3], rest[-3:]
    blocks = owner_ref.shape[0]
    group_size = used_ref.shape[0]
    width = mass_ref.shape[1]
    half_rows = payload_refs[0].shape[1]
    half_width = width // HALVES

    def clear_used(i, carry):
        used_ref[i] = 0
        return carry

    lax.fori_loop(0, group_size, clear_used, 0)
    lane = lax.broadcasted_iota(jnp.int32, (1, width), 1)

    def clear_marks(i, carry):
        for payload_ref in payload_refs:
            payload_ref[i, 16:32, :] = jnp.full((16, LANES), -1.0, BF16)
        return carry

    lax.fori_loop(0, payload_refs[0].shape[0], clear_marks, 0)

    def pack(block, carry):
        owner = owner_ref[block]
        rank = used_ref[owner]
        used_ref[owner] = rank + 1
        chunk = rank // portion
        where = owner * portion + rank % portion
        dest_ref[block] = chunk * (group_size * portion) + where
        count = count_ref[block]
        mark = slot_ref[block].astype(F32)
        cols = pl.ds(pl.multiple_of(block * width, LANES), width)
        live = jnp.where(lane < count, mass_ref[pl.ds(block, 1), :], 0.0)
        velocity = velocity_ref[:, cols]
        affine = affine_ref[:, cols]
        code = cell_ref[:, cols] * QUANT + fraction_ref[:, cols]
        high = (code >> 7).astype(F32)
        low = (code & 127).astype(F32)
        for q in range(width // LANES):
            part = slice(q * LANES, (q + 1) * LANES)
            first_lane = q * LANES // half_width * half_width
            base = q * FIELDS
            stage_ref[base : base + 1] = live[:, part]
            stage_ref[base + 1 : base + 4] = velocity[:, part]
            stage_ref[base + 4 : base + 13] = affine[:, part]
            stage_ref[base + 13 : base + 16] = high[:, part]
            stage_ref[base + 16 : base + 19] = low[:, part]
            stage_ref[base + 19 : base + 20] = jnp.full(
                (1, LANES), jnp.where(count > first_lane, mark, -1.0), F32
            )
        for c, payload_ref in enumerate(payload_refs):

            @pl.when(chunk == c)
            def _():
                for h in range(HALVES):
                    payload_ref[where * HALVES + h] = stage_ref[
                        h * half_rows : (h + 1) * half_rows
                    ].astype(BF16)

        return carry

    lax.fori_loop(0, blocks, pack, 0)


def pack(chunks, portion, group_size, owner, slot, count, mass, velocity, affine, cell, fraction):
    blocks = owner.shape[0]
    width = mass.shape[0] // blocks
    rows = width // LANES * FIELDS
    payload = jax.ShapeDtypeStruct(
        (group_size * portion * HALVES, rows // HALVES, LANES), BF16
    )
    outs = pl.pallas_call(
        functools.partial(pack_kernel, portion),
        name="pack",
        out_shape=(payload,) * chunks + (jax.ShapeDtypeStruct((blocks,), jnp.int32),),
        in_specs=[SMEM] * 3 + [VMEM] * 5,
        out_specs=(VMEM,) * chunks + (SMEM,),
        scratch_shapes=[pltpu.SMEM((group_size,), jnp.int32), pltpu.VMEM((rows, LANES), F32)],
        compiler_params=PARAMS,
    )(owner, slot, count, mass.reshape(blocks, width), velocity, affine, cell, fraction)
    return outs[:-1], outs[-1]


def twice(rows):
    return jnp.concatenate([rows, rows], axis=0)


def load_item(u, item_ref, fields_ref):
    rows = item_ref.shape[0]
    quarters = rows // FIELDS
    first = u * rows
    fields_ref[first : first + rows] = item_ref[...].astype(F32)
    for q in range(quarters):
        base = first + q * FIELDS
        fields_ref[base + 13 : base + 16] = (
            fields_ref[base + 13 : base + 16] * (128.0 / QUANT)
            + fields_ref[base + 16 : base + 19] * (1.0 / QUANT)
            + (0.5 + 0.5 / QUANT)
        )

    def spread(field):
        return twice(
            jnp.concatenate(
                [
                    fields_ref[pl.ds(first + q * FIELDS + field, 8, stride=0), :]
                    for q in range(quarters)
                ],
                axis=1,
            )
        )

    return spread, quarters


def stencil(spread, node, dim):
    offset = node - spread(13 + dim)
    magnitude = jnp.abs(offset)
    outer_part = jnp.maximum(1.5 - magnitude, 0.0)
    weight = jnp.where(
        magnitude < 0.5, 0.75 - magnitude * magnitude, 0.5 * outer_part * outer_part
    )
    return weight, weight * offset


def planes(u, spread, quarters, node, rows_ref):
    factors_y = stencil(spread, node, 1)
    factors_z = [factor.astype(BF16) for factor in stencil(spread, node, 2)]
    firsts = [(u * 2 + k) * quarters * EDGE for k in range(2)]
    for first, factor in zip(firsts, factors_y):
        for q in range(quarters):
            rows_ref[first + q * EDGE : first + (q + 1) * EDGE] = factor[
                :, q * LANES : (q + 1) * LANES
            ]

    def row(first, y):
        return jnp.concatenate(
            [
                twice(rows_ref[pl.ds(first + q * EDGE + y, 8, stride=0), :]).astype(BF16)
                for q in range(quarters)
            ],
            axis=1,
        )

    zero, one, two = [], [], []
    for y in range(EDGE):
        weight_row, slope_row = row(firsts[0], y), row(firsts[1], y)
        zero.append(weight_row * factors_z[0])
        one.append(slope_row * factors_z[0])
        two.append(weight_row * factors_z[1])
    return [jnp.concatenate(parts, axis=0) for parts in (zero, one, two)]


def nodes(quarters):
    return lax.broadcasted_iota(jnp.int32, (EDGE, quarters * LANES), 0).astype(F32)


def deposit(u, item_ref, fields_ref, rows_ref):
    spread, quarters = load_item(u, item_ref, fields_ref)
    node = nodes(quarters)
    weight_x, slope_x = stencil(spread, node, 0)
    mass = spread(0)
    mass_x = mass * weight_x
    mass_slope = mass * slope_x
    nothing = jnp.zeros(mass_x.shape, BF16)
    lead_zero, lead_one, lead_two = [mass_x.astype(BF16)], [nothing], [nothing]
    for d in range(3):
        lead_zero.append(
            (spread(1 + d) * mass_x + spread(4 + 3 * d) * mass_slope).astype(BF16)
        )
        lead_one.append((spread(5 + 3 * d) * mass_x).astype(BF16))
        lead_two.append((spread(6 + 3 * d) * mass_x).astype(BF16))
    lead = jnp.concatenate(
        [jnp.concatenate(part, axis=0) for part in (lead_zero, lead_one, lead_two)], axis=1
    )
    plane = jnp.concatenate(planes(u, spread, quarters, node, rows_ref), axis=1)
    return lax.dot_general(lead, plane, (((1,), (1,)), ((), ())), preferred_element_type=F32)


def interpolate(u, item_ref, grid_rows, fields_ref, rows_ref, parts_ref):
    spread, quarters = load_item(u, item_ref, fields_ref)
    node = nodes(quarters)
    weight_x, slope_x = stencil(spread, node, 0)
    moments = [
        jnp.dot(grid_rows, plane, preferred_element_type=F32)
        for plane in planes(u, spread, quarters, node, rows_ref)
    ]
    slope_four = 4.0 * slope_x
    weight_four = 4.0 * weight_x
    first = u * quarters * RESULTS * 8
    for d in range(3):
        span = slice(d * EDGE, (d + 1) * EDGE)
        entries = (
            (d, weight_x, moments[0]),
            (3 + 3 * d, slope_four, moments[0]),
            (4 + 3 * d, weight_four, moments[1]),
            (5 + 3 * d, weight_four, moments[2]),
        )
        for entry, factor, moment in entries:
            product = factor * moment[span]
            partial = product[:8] + product[8:]
            for q in range(quarters):
                at = first + (q * RESULTS + entry) * 8
                parts_ref[at : at + 8] = partial[:, q * LANES : (q + 1) * LANES]
    groups = []
    for g in range(quarters * RESULTS // 8):
        total = parts_ref[pl.ds(first + g * 64, 8, stride=8), :]
        for j in range(1, 8):
            total = total + parts_ref[pl.ds(first + g * 64 + j, 8, stride=8), :]
        groups.append(total)
    return jnp.concatenate(groups, axis=0).astype(BF16)


def collect_filled(tiles_ref, order_ref):
    def collect(s, filled):
        order_ref[filled] = s
        return filled + (tiles_ref[s] >= 0).astype(jnp.int32)

    order_ref[0] = 0
    filled = lax.fori_loop(0, tiles_ref.shape[0], collect, 0)
    last = order_ref[jnp.maximum(filled - 1, 0)]
    for u in range(UNROLL):
        order_ref[filled + u] = last
    return filled


def scatter_items(tiles_ref, arrived_ref, sums_ref, order_ref, fields_ref, rows_ref):
    filled = collect_filled(tiles_ref, order_ref)
    spare = sums_ref.shape[0] - 1

    def scatter(step, carry):
        results = []
        for u in range(UNROLL):
            at = step * UNROLL + u
            s = order_ref[at]
            tile = jnp.where(at < filled, tiles_ref[s], spare)
            results.append((tile, deposit(u, arrived_ref.at[s], fields_ref, rows_ref)))
        for tile, sums in results:
            sums_ref[tile] += sums
        return carry

    lax.fori_loop(0, (filled + UNROLL - 1) // UNROLL, scatter, 0)


def gather_items(
    tiles_ref, arrived_ref, round_ref, out_ref, order_ref, fields_ref, rows_ref, parts_ref
):
    filled = collect_filled(tiles_ref, order_ref)

    def gather(step, carry):
        for u in range(UNROLL):
            s = order_ref[step * UNROLL + u]
            out_ref[s] = interpolate(
                u,
                arrived_ref.at[s],
                round_ref[jnp.maximum(tiles_ref[s], 0)],
                fields_ref,
                rows_ref,
                parts_ref,
            )
        return carry

    lax.fori_loop(0, (filled + UNROLL - 1) // UNROLL, gather, 0)


def work_shapes(slots, item_rows):
    quarters = item_rows // FIELDS
    return [
        pltpu.SMEM((slots + UNROLL,), jnp.int32),
        pltpu.VMEM((UNROLL * item_rows, LANES), F32),
        pltpu.VMEM((UNROLL * 2 * quarters * EDGE, LANES), F32),
        pltpu.VMEM((UNROLL * quarters * RESULTS * 8, LANES), F32),
    ]


def start_kernel(drag_ref, sums_ref):
    plane_size = EDGE * EDGE

    def start(t, carry):
        for x in range(EDGE):
            sums_ref[t, x : x + 1, :] = drag_ref[
                pl.ds(t, 1), x * plane_size : (x + 1) * plane_size
            ]
        sums_ref[t, EDGE:, :] = jnp.zeros((3 * EDGE, plane_size), F32)
        return carry

    lax.fori_loop(0, drag_ref.shape[0], start, 0)
    sums_ref[drag_ref.shape[0]] = jnp.zeros((4 * EDGE, plane_size), F32)


def start_sums(drag):
    return pl.pallas_call(
        start_kernel,
        name="start_sums",
        out_shape=jax.ShapeDtypeStruct((drag.shape[0] + 1, 4 * EDGE, EDGE * EDGE), F32),
        in_specs=[VMEM],
        out_specs=VMEM,
        compiler_params=PARAMS,
        cost_estimate=cost(1 << 20),
    )(drag)


def copy_sums(before_ref, sums_ref):
    def copy(t, carry):
        sums_ref[t] = before_ref[t]
        return carry

    lax.fori_loop(0, sums_ref.shape[0], copy, 0)


def scatter_kernel(
    tiles_ref, arrived_ref, before_ref, sums_ref, order_ref, fields_ref, rows_ref, parts_ref
):
    copy_sums(before_ref, sums_ref)
    scatter_items(tiles_ref, arrived_ref, sums_ref, order_ref, fields_ref, rows_ref)


def scatter_step(tiles, arrived, sums):
    return pl.pallas_call(
        scatter_kernel,
        name="scatter_step",
        out_shape=jax.ShapeDtypeStruct(sums.shape, F32),
        in_specs=[SMEM, VMEM, VMEM],
        out_specs=VMEM,
        scratch_shapes=work_shapes(arrived.shape[0], arrived.shape[1]),
        compiler_params=PARAMS,
        cost_estimate=cost(10**10),
    )(tiles, arrived, sums)


def grid_kernel(
    last_tiles_ref,
    last_ref,
    tiles_ref,
    arrived_ref,
    before_ref,
    grid_ref,
    round_ref,
    out_ref,
    order_ref,
    fields_ref,
    rows_ref,
    parts_ref,
    sums_ref,
):
    plane_size = EDGE * EDGE
    copy_sums(before_ref, sums_ref)
    scatter_items(last_tiles_ref, last_ref, sums_ref, order_ref, fields_ref, rows_ref)

    def divide(t, carry):
        mass = sums_ref[t, :EDGE, :]
        parts = [sums_ref[t, (d + 1) * EDGE : (d + 2) * EDGE, :] / mass for d in range(3)]
        round_ref[t] = jnp.concatenate(parts, axis=0).astype(BF16)
        for d in range(3):
            for x in range(EDGE):
                grid_ref[t, d : d + 1, x * plane_size : (x + 1) * plane_size] = parts[d][
                    x : x + 1
                ]
        return carry

    lax.fori_loop(0, round_ref.shape[0], divide, 0)
    gather_items(
        tiles_ref, arrived_ref, round_ref, out_ref, order_ref, fields_ref, rows_ref, parts_ref
    )


def result_shape(arrived):
    slots, rows, _ = arrived.shape
    return jax.ShapeDtypeStruct((slots, rows // FIELDS * RESULTS, LANES), BF16)


def grid_step(last_tiles, last, tiles, arrived, sums):
    tile_count = sums.shape[0] - 1
    plane_size = EDGE * EDGE
    return pl.pallas_call(
        grid_kernel,
        name="grid_step",
        out_shape=(
            jax.ShapeDtypeStruct((tile_count, 3, EDGE * plane_size), F32),
            jax.ShapeDtypeStruct((tile_count, 3 * EDGE, plane_size), BF16),
            result_shape(arrived),
        ),
        in_specs=[SMEM, VMEM, SMEM, VMEM, VMEM],
        out_specs=(VMEM,) * 3,
        scratch_shapes=work_shapes(arrived.shape[0], arrived.shape[1])
        + [pltpu.VMEM(sums.shape, F32)],
        compiler_params=PARAMS,
        cost_estimate=cost(10**10),
    )(last_tiles, last, tiles, arrived, sums)


def gather_step(tiles, arrived, rounded):
    return pl.pallas_call(
        gather_items,
        name="gather_step",
        out_shape=result_shape(arrived),
        in_specs=[SMEM, VMEM, VMEM],
        out_specs=VMEM,
        scratch_shapes=work_shapes(arrived.shape[0], arrived.shape[1]),
        compiler_params=PARAMS,
        cost_estimate=cost(10**10),
    )(tiles, arrived, rounded)


def unpack_kernel(dest_ref, count_ref, *refs):
    returned_refs, (velocity_ref, affine_ref) = refs[:-2], refs[-2:]
    blocks = dest_ref.shape[0]
    width = velocity_ref.shape[1] // blocks
    slots = returned_refs[0].shape[0] // HALVES
    half_width = width // HALVES
    lane = lax.broadcasted_iota(jnp.int32, (1, LANES), 1)

    def unpack(block, carry):
        dest = dest_ref[block]
        count = count_ref[block]
        for c, returned_ref in enumerate(returned_refs):

            @pl.when(dest // slots == c)
            def _():
                for h in range(HALVES):
                    rows = returned_ref[(dest - c * slots) * HALVES + h].astype(F32)
                    for q in range(half_width // LANES):
                        first = h * half_width + q * LANES
                        cols = pl.ds(pl.multiple_of(block * width + first, LANES), LANES)
                        part = jnp.where(
                            lane + first < count, rows[q * RESULTS : (q + 1) * RESULTS], 0.0
                        )
                        velocity_ref[:, cols] = part[:3]
                        affine_ref[:, cols] = part[3:]

        return carry

    lax.fori_loop(0, blocks, unpack, 0)


def unpack(dest, count, returned, width):
    particles = dest.shape[0] * width
    return pl.pallas_call(
        unpack_kernel,
        name="unpack",
        out_shape=(
            jax.ShapeDtypeStruct((3, particles), F32),
            jax.ShapeDtypeStruct((9, particles), F32),
        ),
        in_specs=[SMEM, SMEM] + [VMEM] * len(returned),
        out_specs=(VMEM, VMEM),
        compiler_params=PARAMS,
    )(dest, count, *returned)


def tile_marks(arrived):
    return arrived[:, FIELDS - 1, 0].astype(jnp.int32)


def exchange(value):
    return lax.all_to_all(value, GROUP_AXES, split_axis=0, concat_axis=0, tiled=True)


def per_device(
    particle_mass,
    particle_velocity,
    particle_affine,
    particle_cell,
    particle_fraction,
    block_owner,
    block_slot,
    block_count,
    cell_drag,
):
    group_size = lax.axis_size(GROUP_AXES)
    blocks = block_count.shape[0]
    capacity = max(1, 2 * blocks // group_size)
    chunks = 2 if capacity % 2 == 0 else 1
    portion = capacity // chunks
    payloads, dest = pack(
        chunks,
        portion,
        group_size,
        block_owner[:, 0],
        block_slot,
        block_count,
        particle_mass,
        particle_velocity,
        particle_affine,
        particle_cell,
        particle_fraction,
    )
    arrived = [exchange(payload) for payload in payloads]
    tiles = [tile_marks(part) for part in arrived]
    sums = start_sums(cell_drag)
    for c in range(chunks - 1):
        sums = scatter_step(tiles[c], arrived[c], sums)
    grid_velocity, rounded, results = grid_step(
        tiles[-1], arrived[-1], tiles[0], arrived[0], sums
    )
    returned = [exchange(results)]
    for c in range(1, chunks):
        returned.append(exchange(gather_step(tiles[c], arrived[c], rounded)))
    new_velocity, new_affine = unpack(
        dest, block_count, returned, particle_mass.shape[0] // blocks
    )
    return grid_velocity, new_velocity, new_affine


def solution(mesh):
    everywhere = ("gx", "gy", "gz")
    return jax.shard_map(
        per_device,
        mesh=mesh,
        in_specs=(
            P(everywhere),
            P(None, everywhere),
            P(None, everywhere),
            P(None, everywhere),
            P(None, everywhere),
            P(everywhere, None),
            P(everywhere),
            P(everywhere),
            P(everywhere, None),
        ),
        out_specs=(P(everywhere, None, None), P(None, everywhere), P(None, everywhere)),
        check_vma=False,
    )
```

time: 213 us -> 198 us (0.930); the launches traced: 215 us -> 197 us
  waiting for transfers between devices: 90 us -> 58.4 us
  blocking collectives: 10.2 us -> 36.7 us
  starting transfers between devices: 47.5 us -> 30.1 us
  other arithmetic: 0.67 us -> 5.66 us
    all_to_all x2 -> x3, waiting for transfers between devices: 90 us -> 58.4 us  [exchange(): lax.all_to_all(value, GROUP_AXES, split_axis=0, concat_axis=0, tiled=True)]
    all_to_all x1, blocking collectives: 10.2 us -> 36.7 us  [exchange(): lax.all_to_all(value, GROUP_AXES, split_axis=0, concat_axis=0, tiled=True)]
    pallas_call x1, Pallas kernels: 45.6 us -> 20.1 us  [grid_step(): pl.pallas_call(grid_kernel, name='grid_step', out_shape=(jax.ShapeDtypeSt...]
    pallas_call x1 -> x4, Pallas kernels: 4.28 us -> 29.4 us  [the longest x1 20.2 us: scatter_step(): pl.pallas_call(scatter_kernel, name='scatter_step', out_shape=jax.ShapeDt...]
    all_to_all x2 -> x3, starting transfers between devices: 47.5 us -> 30.1 us  [exchange(): lax.all_to_all(value, GROUP_AXES, split_axis=0, concat_axis=0, tiled=True)]
    convert_element_type x0 -> x2, other arithmetic: none -> 5.66 us  [tile_marks(): return arrived[:, FIELDS - 1, 0].astype(jnp.int32)]
    unnamed x21 -> x19, local copies, waits for them, and re-layouts: 11.7 us -> 11.1 us
  transfers between devices with their start and end apart: 2 -> 3, of which waited for: 2 -> 3; matrix products, arithmetic and copies ran while one was open for 2% -> 3% of each run, Pallas kernels for 0% -> 2%
where the time goes in v2:
time: 198 us; the launch traced here: 197 us
  waiting for transfers between devices  58.4 us (29%)
  Pallas kernels  53.4 us (27%)
  blocking collectives  36.7 us (19%)
  starting transfers between devices  30.1 us (15%)
  local copies, waits for them, and re-layouts  12.1 us (6%)
  other arithmetic  5.66 us (3%)
    all_to_all x3, waiting for transfers between devices, exchange(): lax.all_to_all(value, GROUP_AXES, split_axis=0, concat_axis=0, tiled=True)  58.4 us
    all_to_all x1, blocking collectives, exchange(): lax.all_to_all(value, GROUP_AXES, split_axis=0, concat_axis=0, tiled=True)  36.7 us
    all_to_all x3, starting transfers between devices, exchange(): lax.all_to_all(value, GROUP_AXES, split_axis=0, concat_axis=0, tiled=True)  30.1 us
    pallas_call x1, Pallas kernels, scatter_step(): pl.pallas_call(scatter_kernel, name='scatter_step', out_shape=jax.ShapeDt...  20.2 us
    pallas_call x1, Pallas kernels, grid_step(): pl.pallas_call(grid_kernel, name='grid_step', out_shape=(jax.ShapeDtypeSt...  20.1 us
    unnamed x19, local copies, waits for them, and re-layouts  11.1 us
    convert_element_type x2, other arithmetic, tile_marks(): return arrived[:, FIELDS - 1, 0].astype(jnp.int32)  5.66 us
    pallas_call x1, Pallas kernels, pack(): pl.pallas_call(functools.partial(pack_kernel, portion), name='pack', out_...  5.56 us
  transfers between devices with their start and end apart: 3, of which 3 were waited for; matrix products, arithmetic and copies ran while one was open for 3% of the time, Pallas kernels for 2%

profile of v2, /device:TPU:13, one launch (start us, length us, event | category | flops | bytes accessed | tf_op | source)
XLA Modules:
  0.0 197.1 jit_solution(10723891723402035019)
XLA Ops:
  0.6 0.9 reshape.13.mass_ref
  1.6 0.0 copy-start
  1.6 1.0 copy-done
  2.6 0.0 copy-start.1
  2.6 1.0 copy-done.1
  3.6 0.0 copy-start.2
  3.6 1.0 copy-done.2
  4.7 0.0 copy-start.4
  4.7 0.7 copy-done.4
  5.3 0.0 copy-start.6
  5.3 0.7 copy-done.6
  6.0 0.7 copy-done.7
  6.7 5.6 %pack.1 = (bf16[128,40,128]{2,1,0:T(8,128)(2,1)}, bf16[128,40,128]{2,1,0:T(8,128)(2,1)S(1)}, s32[64]{0:T(128)S(1)}) custom-call(s32[64]{0:T(128)S(1)} %bitcast.1, s32[64]{0:T(128)S(1)} %copy-done.7, s32[64]{0:T(128)S(1)} %copy-done.4, f32[64,512]{1,0:T(8,128)S(1)} %reshape.13.mass_ref, f32[3,32768]{1,0:T(4,128)S(1)} %copy-done, f32[9,32768]{1,0:T(8,128)} %affine_ref.1, ...), custom_call_target="tpu_custom_call" | custom-call | tf_op jit(solution)/shard_map/pack/pallas_call | solution.py:113
  12.2 36.7 %all_to_all.20.last_ref.arrived_ref = bf16[128,40,128]{2,1,0:T(8,128)(2,1)S(1)} all-to-all(bf16[128,40,128]{2,1,0:T(8,128)(2,1)S(1)} %get-tuple-element.11), channel_id=1, replica_groups=mesh['gx'=2,'gy'=4,'gz'=4] {'gy','gz'}, dimensions={0} | all-to-all | bytes 2621440 | tf_op jit(solution)/shard_map/all_to_all | solution.py:496
  49.0 5.2 %all-to-all-start.1 = ((bf16[128,40,128]{2,1,0:T(8,128)(2,1)}), bf16[128,40,128]{2,1,0:T(8,128)(2,1)}, u32[]{:S(2)}, u32[]{:S(2)}) async-start(bf16[128,40,128]{2,1,0:T(8,128)(2,1)} %get-tuple-element.12), calls=%async_computation.1 | async-start | bytes 2621440 | tf_op jit(solution)/shard_map/all_to_all | solution.py:496
  54.2 1.0 copy-done.3
  55.2 0.5 start_sums.1.before_ref
  55.7 2.4 %fusion.1.last_tiles_ref.tiles_ref = s32[128]{0:T(128)S(1)} fusion(bf16[128,40,128]{2,1,0:T(8,128)(2,1)S(1)} %all_to_all.20.last_ref.arrived_ref), kind=kLoop, calls=%fused_computation.3 | loop fusion | flops 128 | bytes 768 | tf_op jit(solution)/shard_map/convert_element_type | solution.py:492
  58.0 26.8 %all-to-all-done.1.arrived_ref = bf16[128,40,128]{2,1,0:T(8,128)(2,1)} async-done(((bf16[128,40,128]{2,1,0:T(8,128)(2,1)}), bf16[128,40,128]{2,1,0:T(8,128)(2,1)}, u32[]{:S(2)}, u32[]{:S(2)}) %all-to-all-start.1) | async-done | bytes 1310752 | tf_op jit(solution)/shard_map/all_to_all | solution.py:496
  84.8 3.3 %fusion.tiles_ref = s32[128]{0:T(128)S(1)} fusion(bf16[128,40,128]{2,1,0:T(8,128)(2,1)} %all-to-all-done.1.arrived_ref), kind=kLoop, calls=%fused_computation.1 | loop fusion | flops 128 | bytes 768 | tf_op jit(solution)/shard_map/convert_element_type | solution.py:492
  88.2 20.2 %scatter_step.1.before_ref = f32[33,64,256]{2,1,0:T(8,128)S(1)} custom-call(s32[128]{0:T(128)S(1)} %fusion.tiles_ref, bf16[128,40,128]{2,1,0:T(8,128)(2,1)} %all-to-all-done.1.arrived_ref, f32[33,64,256]{2,1,0:T(8,128)S(1)} %start_sums.1.before_ref), custom_call_target="tpu_custom_call" | custom-call | flops 10000000000 | bytes 4194304 | tf_op jit(solution)/shard_map/scatter_step/pallas_call | solution.py:359
  108.3 0.0 copy-start.8
  108.3 1.3 copy-done.8
  109.7 20.1 %grid_step.1 = (f32[32,3,4096]{2,1,0:T(4,128)}, bf16[32,48,256]{2,1,0:T(8,128)(2,1)S(1)}, bf16[128,24,128]{2,1,0:T(8,128)(2,1)}) custom-call(s32[128]{0:T(128)S(1)} %fusion.1.last_tiles_ref.tiles_ref, bf16[128,40,128]{2,1,0:T(8,128)(2,1)S(1)} %all_to_all.20.last_ref.arrived_ref, s32[128]{0:T(128)S(1)} %fusion.tiles_ref, ...), custom_call_target="tpu_custom_call" | custom-call | flops 10000000000 | bytes 4194304 | tf_op jit(solution)/shard_map/grid_step/pallas_call | solution.py:415
  129.8 20.1 %all-to-all-start.2 = ((bf16[128,24,128]{2,1,0:T(8,128)(2,1)}), bf16[128,24,128]{2,1,0:T(8,128)(2,1)S(1)}, u32[]{:S(2)}, u32[]{:S(2)}) async-start(bf16[128,24,128]{2,1,0:T(8,128)(2,1)} %get-tuple-element.15), calls=%async_computation.2 | async-start | bytes 1572864 | tf_op jit(solution)/shard_map/all_to_all | solution.py:496
  149.8 3.2 %gather_step.1 = bf16[128,24,128]{2,1,0:T(8,128)(2,1)} custom-call(s32[128]{0:T(128)S(1)} %fusion.1.last_tiles_ref.tiles_ref, bf16[128,40,128]{2,1,0:T(8,128)(2,1)S(1)} %all_to_all.20.last_ref.arrived_ref, bf16[32,48,256]{2,1,0:T(8,128)(2,1)S(1)} %get-tuple-element.16.round_ref), custom_call_target="tpu_custom_call" | custom-call | flops 10000000000 | bytes 4194304 | tf_op jit(solution)/shard_map/gather_step/pallas_call | solution.py:433
  153.0 16.1 %all-to-all-done.2.refs_0_ = bf16[128,24,128]{2,1,0:T(8,128)(2,1)S(1)} async-done(((bf16[128,24,128]{2,1,0:T(8,128)(2,1)}), bf16[128,24,128]{2,1,0:T(8,128)(2,1)S(1)}, u32[]{:S(2)}, u32[]{:S(2)}) %all-to-all-start.2) | async-done | bytes 786464 | tf_op jit(solution)/shard_map/all_to_all | solution.py:496
  169.1 4.8 %all-to-all-start.3 = ((bf16[128,24,128]{2,1,0:T(8,128)(2,1)}), bf16[128,24,128]{2,1,0:T(8,128)(2,1)S(1)}, u32[]{:S(2)}, u32[]{:S(2)}) async-start(bf16[128,24,128]{2,1,0:T(8,128)(2,1)} %gather_step.1), calls=%async_computation.3 | async-start | bytes 1572864 | tf_op jit(solution)/shard_map/all_to_all | solution.py:496
  173.9 3.7 %copy.13 = f32[32,3,4096]{2,0,1:T(8,128)} copy(f32[32,3,4096]{2,1,0:T(4,128)} %get-tuple-element.22) | data formatting | bytes 3145728
  177.6 15.6 %all-to-all-done.3.refs_1_ = bf16[128,24,128]{2,1,0:T(8,128)(2,1)S(1)} async-done(((bf16[128,24,128]{2,1,0:T(8,128)(2,1)}), bf16[128,24,128]{2,1,0:T(8,128)(2,1)S(1)}, u32[]{:S(2)}, u32[]{:S(2)}) %all-to-all-start.3) | async-done | bytes 786464 | tf_op jit(solution)/shard_map/all_to_all | solution.py:496
  193.1 0.0 copy-done.5
  193.1 3.9 %unpack.1 = (f32[3,32768]{1,0:T(4,128)}, f32[9,32768]{1,0:T(8,128)}) custom-call(s32[64]{0:T(128)S(1)} %get-tuple-element.14.dest_ref, s32[64]{0:T(128)S(1)} %copy-done.5, bf16[128,24,128]{2,1,0:T(8,128)(2,1)S(1)} %all-to-all-done.2.refs_0_, bf16[128,24,128]{2,1,0:T(8,128)(2,1)S(1)} %all-to-all-done.3.refs_1_), custom_call_target="tpu_custom_call" | custom-call | tf_op jit(solution)/shard_map/unpack/pallas_call | solution.py:478
  (3 shorter events, 0.0 us)
Async XLA Ops:
  1.6 1.0 copy-start
  2.6 1.0 copy-start.1
  3.6 1.0 copy-start.2
  4.7 0.7 copy-start.4
  5.3 0.7 copy-start.6
  6.0 0.7 copy-start.7
  49.0 35.9 %all-to-all-start.1 = ((bf16[128,40,128]{2,1,0:T(8,128)(2,1)}), bf16[128,40,128]{2,1,0:T(8,128)(2,1)}, u32[]{:S(2)}, u32[]{:S(2)}) async-start(bf16[128,40,128]{2,1,0:T(8,128)(2,1)} %get-tuple-element.12), calls=%async_computation.1 | async-start | bytes 2621440 | tf_op jit(solution)/shard_map/all_to_all | solution.py:496
  54.2 1.0 copy-start.3
  108.3 1.4 copy-start.8
  129.8 39.3 %all-to-all-start.2 = ((bf16[128,24,128]{2,1,0:T(8,128)(2,1)}), bf16[128,24,128]{2,1,0:T(8,128)(2,1)S(1)}, u32[]{:S(2)}, u32[]{:S(2)}) async-start(bf16[128,24,128]{2,1,0:T(8,128)(2,1)} %get-tuple-element.15), calls=%async_computation.2 | async-start | bytes 1572864 | tf_op jit(solution)/shard_map/all_to_all | solution.py:496
  169.1 24.1 %all-to-all-start.3 = ((bf16[128,24,128]{2,1,0:T(8,128)(2,1)}), bf16[128,24,128]{2,1,0:T(8,128)(2,1)S(1)}, u32[]{:S(2)}, u32[]{:S(2)}) async-start(bf16[128,24,128]{2,1,0:T(8,128)(2,1)} %gather_step.1), calls=%async_computation.3 | async-start | bytes 1572864 | tf_op jit(solution)/shard_map/all_to_all | solution.py:496
  173.9 19.2 %copy-start.5 = (s32[64]{0:T(128)S(1)}, s32[64]{0:T(128)}, u32[]{:S(2)}) copy-start(s32[64]{0:T(128)} %count_ref.3) | copy-start | bytes 772
